TPU v7x, 128 devices: a whole 4x4x4 slice. The times are simulated.
128 devices in a mesh: row: 8 (over x, core), col: 16 (over z, y).
Axes of the slice: x: 4, y: 4, z: 4, core: 2. Of those that a mesh axis runs over, the one named last changes fastest.
Arguments:
- coords: float32 [3, 2097152], P(None, ('row', 'col')), may hold values from 0 to 6
- vectors: bfloat16 [64, 2097152], P(None, ('row', 'col')), may hold values from -0.59765625 to 0.59765625
- basis: bfloat16 [32, 2097152], P(None, ('row', 'col')), may hold values from -1.5 to 1.5
- transfer: float32 [32, 262144], P(None, ('row', 'col')), may hold values from -0.3 to 0.3
- leaf_skeleton: float32 [3, 262144], P(None, ('row', 'col')), may hold values from 0 to 6
- device_skeleton: float32 [3, 4096], P(None, ('row', 'col')), may hold values from 0 to 6
- near_pairs: int32 [2, 49152], P(None, ('row', 'col')), may hold values from 0 to 8191, as said below
- far_leaves: int32 [8192, 8], P(('row', 'col')), may hold values from 0 to 8191, as said below
- far_devices: int32 [128, 16], P(('row', 'col')), may hold values from 0 to 127
Outputs:
- product: float32 [64, 2097152], P(None, ('row', 'col'))
Inputs may be any that keep to these rules, and one draw needn't show every extreme that they name: `near_pairs`: device k of the row x col grid (k = row index * 16 + col index) holds near blocks k * 6 * 64 to (k + 1) * 6 * 64 - 1 and leaves k * 64 to (k + 1) * 64 - 1; the target and the source leaf of each of its near blocks lie on device k or on a device beside it in the grid, diagonals included. `far_leaves`: the coupling partners of a leaf lie on that leaf's device or on a device beside it in the row x col grid, diagonals included.
All inputs are finite; a program needn't handle non-finite values.
Results may differ from a plain program's by a relative error of at most 0.004.
Values may be sent and summed in bfloat16 or wider, within the bound.
A program may use at most 256 MiB of HBM per device.

v0:
```python
import math
import jax
import jax.numpy as jnp
from jax import lax
from jax.sharding import PartitionSpec as P

HIGH = lax.Precision.HIGHEST


def with_halo(array, sides, width):
    for axis, dim in sides:
        devices, length = (lax.axis_size(axis), array.shape[dim])
        up = [(i, (i + 1) % devices) for i in range(devices - 1)]
        down = [(j, i) for i, j in up]
        last = lax.slice_in_dim(array, length - width, length, axis=dim)
        initial = lax.slice_in_dim(array, 0, width, axis=dim)
        before = lax.ppermute(last, axis, up)
        after = lax.ppermute(initial, axis, down)
        array = jnp.concatenate([before, array, after], axis=dim)
    return array


def from_behind(block, axis, distance):
    devices = range(lax.axis_size(axis))
    route = [(i - distance, i) for i in devices if i - distance in devices]
    return lax.ppermute(block, axis, route)


def turned_gather(arrays, axis, dims):
    turned = [jnp.moveaxis(a, dim, 0) for a, dim in zip(arrays, dims)]
    both = jnp.concatenate([t.reshape(len(t), -1) for t in turned], axis=1)
    result, at, outs = (lax.all_gather(both, axis, axis=0, tiled=True), 0, [])
    for t, dim in zip(turned, dims):
        share = result[:, at : at + t[0].size].reshape(-1, *t.shape[1:])
        outs.append(jnp.moveaxis(share, 0, dim))
        at += t[0].size
    return tuple(outs)


def kernel_block(left, right):
    total = None
    for dimension in range(3):
        gap = left[..., dimension, :, None] - right[..., dimension, None, :]
        total = gap * gap if total is None else total + gap * gap
    return jnp.exp(-0.5 * total)


def upsweep(vector_rows, basis_rows):
    return jnp.einsum(
        "nvil,nril->nvir", vector_rows, basis_rows, preferred_element_type=jnp.float32
    ).astype(jnp.bfloat16)


def shards(
    coords,
    vectors,
    basis,
    transfer,
    leaf_skeleton,
    device_skeleton,
    near_pairs,
    far_leaves,
    far_devices,
):
    col_count = lax.axis_size("col")
    row_here = lax.axis_index("row")
    col_here = lax.axis_index("col")
    rank_size = basis.shape[0]
    vec_count = vectors.shape[0]
    leaves = transfer.shape[1] // rank_size
    leaf_width = coords.shape[1] // leaves
    block_group = math.gcd(near_pairs.shape[1], 32)

    def hood_of(global_leaf):
        owner_dev = global_leaf // leaves
        row_offset = owner_dev // col_count - row_here + 1
        col_offset = owner_dev % col_count - col_here + 1
        return (row_offset * 3 + col_offset, global_leaf % leaves)

    points_pad, skeleton_pad = (
        with_halo(coords[None, None], (("row", 0), ("col", 1)), 1),
        with_halo(leaf_skeleton[None, None], (("row", 0), ("col", 1)), 1),
    )
    vectors_pad, basis_pad = (
        with_halo(vectors[None, None], (("row", 0), ("col", 1)), 1),
        with_halo(basis[None, None], (("row", 0), ("col", 1)), 1),
    )
    coeff_pad = upsweep(
        vectors_pad.reshape(9, vec_count, leaves, leaf_width),
        basis_pad.reshape(9, rank_size, leaves, leaf_width),
    )
    coeff_own = coeff_pad[4]
    coords_pool = points_pad.reshape(9, 3, leaves, leaf_width)
    vectors_pool = vectors_pad.reshape(9, vec_count, leaves, leaf_width)
    tgt_hood, tgt_leaf = hood_of(near_pairs[0].reshape(-1, block_group))
    src_hood, src_leaf = hood_of(near_pairs[1].reshape(-1, block_group))

    def near_step(buffer, item):
        t_hood, t_leaf, s_hood, s_leaf = item
        tgt_points = coords_pool[t_hood, :, t_leaf, :]
        src_points = coords_pool[s_hood, :, s_leaf, :]
        block = kernel_block(tgt_points, src_points).astype(jnp.bfloat16)
        src_vectors = vectors_pool[s_hood, :, s_leaf, :]
        partial_value = jnp.einsum(
            "bvs,bts->bvt", src_vectors, block, preferred_element_type=jnp.float32
        )
        return (buffer.at[t_hood, :, t_leaf, :].add(partial_value), None)

    start = jnp.zeros((9, vec_count, leaves, leaf_width), jnp.float32)
    buffer, _ = lax.scan(near_step, start, (tgt_hood, tgt_leaf, src_hood, src_leaf))
    buffer = buffer.reshape(3, 3, vec_count, leaves * leaf_width)
    near_field = buffer[1, 1]
    for row_step in range(3):
        for col_step in range(3):
            if row_step != 1 or col_step != 1:
                offset = (row_step - 1) * col_count + (col_step - 1)
                near_field = near_field + from_behind(
                    buffer[row_step, col_step].astype(jnp.bfloat16), ("row", "col"), offset
                ).astype(jnp.float32)
    far_hood, far_leaf = hood_of(far_leaves)
    picked_coeff = coeff_pad[far_hood, :, far_leaf, :].astype(jnp.float32)
    skeleton_pool = skeleton_pad.reshape(9, 3, leaves, rank_size)
    picked_skel = skeleton_pool[far_hood, :, far_leaf, :]
    own_skel = jnp.transpose(leaf_skeleton.reshape(3, leaves, rank_size), (1, 0, 2))
    coupling = kernel_block(picked_skel, own_skel[:, None])
    leaf_far = jnp.einsum("ifvs,ifst->ivt", picked_coeff, coupling, precision=HIGH)
    transfer_mats = transfer.reshape(rank_size, leaves, rank_size)
    device_coeff = jnp.einsum(
        "vir,ris->vs", coeff_own.astype(jnp.float32), transfer_mats, precision=HIGH
    )
    all_coeffs, all_skeleton = turned_gather(
        (device_coeff, device_skeleton), ("row", "col"), (1, 1)
    )
    chosen = far_devices[0]
    top_coeffs = all_coeffs.reshape(vec_count, -1, rank_size)[:, chosen, :]
    top_skel = jnp.transpose(all_skeleton.reshape(3, -1, rank_size)[:, chosen, :], (1, 0, 2))
    coupling_top = kernel_block(top_skel, device_skeleton[None])
    device_far = jnp.einsum("vfs,fst->vt", top_coeffs, coupling_top, precision=HIGH)
    field = leaf_far + jnp.einsum("vs,ris->ivr", device_far, transfer_mats, precision=HIGH)
    field = field.astype(jnp.bfloat16)
    far_part = jnp.einsum(
        "ivr,ril->vil",
        field,
        basis.reshape(rank_size, leaves, leaf_width),
        preferred_element_type=jnp.float32,
    )
    return near_field + far_part.reshape(vec_count, leaves * leaf_width)


def solution(mesh):
    in_specs = (
        P(None, ("row", "col")),
        P(None, ("row", "col")),
        P(None, ("row", "col")),
        P(None, ("row", "col")),
        P(None, ("row", "col")),
        P(None, ("row", "col")),
        P(None, ("row", "col")),
        P(("row", "col"), None),
        P(("row", "col"), None),
    )
    out_specs = P(None, ("row", "col"))
    return jax.shard_map(shards, mesh=mesh, in_specs=in_specs, out_specs=out_specs, check_vma=False)
```

profile of v0, /device:TPU:1, one launch (start us, length us, event | category | flops | bytes accessed | tf_op | source)
XLA Modules:
  0.0 953.4 jit_solution(7944079981632862380)
XLA Ops:
  7.8 4.5 collective-permute-start.4
  36.9 5.6 collective-permute-start.18
  42.5 10.9 %collective-permute-done.1 = bf16[1,1,64,16384]{3,2,1,0:T(8,128)(2,1)S(1)} collective-permute-done((bf16[1,1,64,16384]{3,2,1,0:T(8,128)(2,1)}, bf16[1,1,64,16384]{3,2,1,0:T(8,128)(2,1)S(1)}, u32[]{:S(2)}, u32[]{:S(2)}) %collective-permute-start.1) | collective-permute-done | bytes 2097184 | tf_op jit(solution)/shard_map/ppermute | solution.py:18
  59.1 6.6 collective-permute-start.2
  70.8 179.7 %collective-permute-done.7 = f32[3,1,3,16384]{3,1,2,0:T(1,128)} collective-permute-done((f32[3,1,3,16384]{3,1,2,0:T(1,128)}, f32[3,1,3,16384]{3,1,2,0:T(1,128)}, u32[]{:S(2)}, u32[]{:S(2)}) %collective-permute-start.7) | collective-permute-done | bytes 589856 | tf_op jit(solution)/shard_map/ppermute | solution.py:18
  255.0 8.6 collective-permute-done.6
  271.3 10.5 %collective-permute-start.20 = (f32[1,1,3,2048]{3,2,1,0:T(4,128)}, f32[1,1,3,2048]{3,2,1,0:T(4,128)}, u32[]{:S(2)}, u32[]{:S(2)}) collective-permute-start(f32[1,1,3,2048]{3,2,1,0:T(4,128)} %bitcast.21), channel_id=1, source_target_pairs={{0,16},{16,32},{32,48},{48,64},{64,80},{80,96},{96,112},{1,17},{17... | collective-permute-start | bytes 73736 | tf_op jit(solution)/shard_map/ppermute | solution.py:17
  281.8 7.8 pad_maximum_fusion.1
  289.6 10.5 %copy.76 = bf16[36,8,64,256]{3,2,1,0:T(8,128)(2,1)} copy(bf16[36,8,64,256]{3,1,2,0:T(8,128)(2,1)} %bitcast.197) | data formatting | bytes 18874368
  300.1 7.1 pad_maximum_fusion
  307.3 4.5 copy.75
  311.8 12.0 %copy.53 = bf16[9,64,64,256]{3,1,2,0:T(8,128)(2,1)} copy(bf16[9,64,64,256]{3,2,1,0:T(8,128)(2,1)S(1)} %bitcast.194) | data formatting | bytes 37748736 | tf_op jit(solution)/shard_map/while | solution.py:110
  323.8 12.6 %broadcast_in_dim.26 = f32[9,64,64,256]{3,1,2,0:T(8,128)} broadcast(f32[]{:T(128)} %constant.129.clone.1), dimensions={} | broadcast | bytes 37748740 | tf_op jit(solution)/shard_map/broadcast_in_dim | solution.py:109
  336.5 303.8 %while.10 = (s32[]{:T(128)}, f32[9,64,64,256]{3,1,2,0:T(8,128)}, s32[12,32]{1,0:T(8,128)S(1)}, s32[12,32]{1,0:T(8,128)S(1)}, s32[12,32]{1,0:T(8,128)S(1)}, /*ind...) while((s32[]{:T(128)}, f32[9,64,64,256]{3,1,2,0:T(8,128)}, ...), condition=%wide.region_2.3_spmd, body=%wide.region_0.2_spmd.sunk | while | flops 289932096 | bytes 12912617 | solution.py:110
  341.4 7.0 gather_fusion
  348.4 7.0 fusion.137
  355.4 6.5 scatter_fusion
  366.7 7.0 gather_fusion
  373.7 7.0 fusion.137
  380.7 6.4 scatter_fusion
  392.1 7.0 gather_fusion
  399.1 7.0 fusion.137
  406.0 6.4 scatter_fusion
  417.4 7.0 gather_fusion
  424.4 7.0 fusion.137
  431.3 6.4 scatter_fusion
  442.7 7.0 gather_fusion
  449.7 7.0 fusion.137
  456.7 6.4 scatter_fusion
  468.0 7.0 gather_fusion
  475.0 7.0 fusion.137
  482.0 6.4 scatter_fusion
  493.3 7.0 gather_fusion
  500.3 7.0 fusion.137
  507.3 6.4 scatter_fusion
  518.6 7.0 gather_fusion
  525.6 7.0 fusion.137
  532.6 6.4 scatter_fusion
  543.9 7.0 gather_fusion
  550.9 7.0 fusion.137
  557.8 6.5 scatter_fusion
  569.2 7.0 gather_fusion
  576.2 7.0 fusion.137
  583.2 6.4 scatter_fusion
  594.5 7.0 gather_fusion
  601.5 7.0 fusion.137
  608.5 6.5 scatter_fusion
  619.9 7.0 gather_fusion
  626.9 7.0 fusion.137
  633.8 6.4 scatter_fusion
  640.3 35.3 %copy.55 = f32[9,64,64,256]{3,2,1,0:T(8,128)} copy(f32[9,64,64,256]{3,1,2,0:T(8,128)} %get-tuple-element.47) | data formatting | bytes 75497472 | tf_op jit(solution)/shard_map/while | solution.py:110
  675.6 40.3 %reshape.193 = f32[3,3,64,16384]{3,2,1,0:T(8,128)} reshape(f32[9,64,64,256]{3,2,1,0:T(8,128)} %copy.55) | data formatting | bytes 75497472 | tf_op jit(solution)/shard_map/reshape | solution.py:111
  715.9 13.1 %convert.10 = bf16[3,3,64,16384]{3,2,1,0:T(8,128)(2,1)S(1)} convert(f32[3,3,64,16384]{3,2,1,0:T(8,128)} %reshape.193) | non-fusion elementwise | flops 9437184 | bytes 56623104 | tf_op jit(solution)/shard_map/convert.7
  729.0 5.9 slice_bitcast_fusion.8
  736.2 6.6 collective-permute-start.15
  744.9 28.9 %convert_bitcast_fusion = bf16[9,64,64,32]{1,3,2,0:T(8,128)(2,1)} fusion(bf16[9,32,64,256]{3,2,1,0:T(8,128)(2,1)} %bitcast.200, bf16[9,64,64,256]{3,2,1,0:T(8,128)(2,1)} %bitcast.195), kind=kOutput, calls=%fused_computation.59 | convolution fusion | flops 605159424 | bytes 30670848 | tf_op jit(solution)/shard_map/nvil,nril->nvir/dot_general | solution.py:49
  779.3 4.1 collective-permute-start.22
  783.4 3.9 collective-permute-done.23
  791.6 8.1 collective-permute-start.13
  801.6 7.0 collective-permute-start.11
  814.1 8.4 gather_fusion.3
  822.5 12.3 %fusion.47 = f32[64,64,32]{1,2,0:T(8,128)S(1)} fusion(bf16[64,8,64,32]{2,3,1,0:T(8,128)(2,1)} %bitcast.199, f32[64,32]{1,0:T(8,128)S(1)} %copy-done.12, f32[64,8,32]{2,1,0:T(8,128)S(1)} %bitcast.222, f32[64,32]{1,0:T(8,128)S(1)} %copy-done.13, f32[64,8,32]{2,1,0:T(8,128)S(1)} %bitcast.221, f32[64,32]{1,0:T(8,128)S(1)} %copy-done.11, ...), kind=kOutput, calls=%fused_computation.88 | convolution fusion | flops 407371776 | bytes 2842624 | tf_op jit(solution)/shard_map/ifvs,ifst->ivt/dot_general | solution.py:126
  834.8 87.4 %all-gather.2.cloned.1.call-done = f32[4096,67]{1,0:T(8,128)} async-done(((f32[32,67]{1,0:T(8,128)}), f32[4096,67]{1,0:T(8,128)}) %all-gather.2.cloned.1.call-update) | async-done | bytes 1097744 | tf_op jit(solution)/shard_map/all_gather | solution.py:32
  936.1 10.2 %fusion.37 = f32[64,16384]{1,0:T(8,128)} fusion(f32[64,16384]{1,0:T(8,128)S(1)} %bitcast.198, f32[3,3,64,16384]{3,2,1,0:T(8,128)} %reshape.193, bf16[64,16384]{1,0:T(8,128)(2,1)} %collective-permute-done.15, bf16[64,16384]{1,0:T(8,128)(2,1)} %collective-permute-done.14, bf16[64,16384]{1,0:T(8,128)(2,1)} %collective-permute-done.13, ...), kind=kLoop, calls=%fused_computation.69 | loop fusion | flops 17825792 | bytes 29360128 | tf_op jit(solution)/shard_map/add | solution.py:147
  (249 shorter events, 141.3 us)
Async XLA Ops:
  6.5 47.8 %copy-start.4 = (bf16[64,16384]{1,0:T(8,128)(2,1)S(1)}, bf16[64,16384]{1,0:T(8,128)(2,1)}, u32[]{:S(2)}) copy-start(bf16[64,16384]{1,0:T(8,128)(2,1)} %param.12) | copy-start | bytes 6291460
  6.5 915.7 %all-gather.2.cloned.1.call-start = ((), (), s32[]{:S(2)}) async-start(), calls=%async_computation | async-start | bytes 2113536 | tf_op jit(solution)/shard_map/all_gather | solution.py:32
  7.8 13.9 %collective-permute-start.4 = (f32[1,1,3,16384]{3,1,2,0:T(1,128)S(1)}, f32[1,1,3,16384]{3,1,2,0:T(1,128)S(1)}, u32[]{:S(2)}, u32[]{:S(2)}) collective-permute-start(f32[1,1,3,16384]{3,1,2,0:T(1,128)S(1)} %broadcast_in_dim.28), channel_id=1, source_target_pairs={{0,16},{16,32},{32,48},{48,64},{64,80},{80,96},{96,112},{1,17},{17... | collective-permute-start | bytes 589832 | tf_op jit(solution)/shard_map/ppermute | solution.py:17
  12.3 53.4 %collective-permute-start.5 = (f32[1,1,3,16384]{3,1,2,0:T(1,128)S(1)}, f32[1,1,3,16384]{3,1,2,0:T(1,128)S(1)}, u32[]{:S(2)}, u32[]{:S(2)}) collective-permute-start(f32[1,1,3,16384]{3,1,2,0:T(1,128)S(1)} %broadcast_in_dim.28), channel_id=1, source_target_pairs={{16,0},{32,16},{48,32},{64,48},{80,64},{96,80},{112,96},{17,1},{33... | collective-permute-start | bytes 589832 | tf_op jit(solution)/shard_map/ppermute | solution.py:18
  14.2 16.3 %collective-permute-start.17 = (bf16[1,1,32,16384]{3,2,1,0:T(8,128)(2,1)}, bf16[1,1,32,16384]{3,2,1,0:T(8,128)(2,1)S(1)}, u32[]{:S(2)}, u32[]{:S(2)}) collective-permute-start(bf16[1,1,32,16384]{3,2,1,0:T(8,128)(2,1)} %bitcast.201), channel_id=1, source_target_pairs={{16,0},{32,16},{48,32},{64,48},{80,64},{96,80},{112,96},{17,1},{33... | collective-permute-start | bytes 3145736 | tf_op jit(solution)/shard_map/ppermute | solution.py:18
  16.1 15.7 %collective-permute-start.16 = (bf16[1,1,32,16384]{3,2,1,0:T(8,128)(2,1)}, bf16[1,1,32,16384]{3,2,1,0:T(8,128)(2,1)S(1)}, u32[]{:S(2)}, u32[]{:S(2)}) collective-permute-start(bf16[1,1,32,16384]{3,2,1,0:T(8,128)(2,1)} %bitcast.202), channel_id=1, source_target_pairs={{0,16},{16,32},{32,48},{48,64},{64,80},{80,96},{96,112},{1,17},{17... | collective-permute-start | bytes 3145736 | tf_op jit(solution)/shard_map/ppermute | solution.py:17
  19.8 33.6 %collective-permute-start.1 = (bf16[1,1,64,16384]{3,2,1,0:T(8,128)(2,1)}, bf16[1,1,64,16384]{3,2,1,0:T(8,128)(2,1)S(1)}, u32[]{:S(2)}, u32[]{:S(2)}) collective-permute-start(bf16[1,1,64,16384]{3,2,1,0:T(8,128)(2,1)} %bitcast.206), channel_id=1, source_target_pairs={{16,0},{32,16},{48,32},{64,48},{80,64},{96,80},{112,96},{17,1},{33... | collective-permute-start | bytes 6291464 | tf_op jit(solution)/shard_map/ppermute | solution.py:18
  21.7 32.6 %collective-permute-start = (bf16[1,1,64,16384]{3,2,1,0:T(8,128)(2,1)}, bf16[1,1,64,16384]{3,2,1,0:T(8,128)(2,1)S(1)}, u32[]{:S(2)}, u32[]{:S(2)}) collective-permute-start(bf16[1,1,64,16384]{3,2,1,0:T(8,128)(2,1)} %bitcast.207), channel_id=1, source_target_pairs={{0,16},{16,32},{32,48},{48,64},{64,80},{80,96},{96,112},{1,17},{17... | collective-permute-start | bytes 6291464 | tf_op jit(solution)/shard_map/ppermute | solution.py:17
  31.8 25.9 %copy-start.7 = (bf16[1,1,32,16384]{3,2,1,0:T(8,128)(2,1)}, bf16[1,1,32,16384]{3,2,1,0:T(8,128)(2,1)S(1)}, u32[]{:S(2)}) copy-start(bf16[1,1,32,16384]{3,2,1,0:T(8,128)(2,1)S(1)} %collective-permute-done.16) | copy-start | bytes 3145732
  35.4 32.3 %copy-start.18 = (s32[2,384]{1,0:T(2,128)S(1)}, s32[2,384]{1,0:T(2,128)}, u32[]{:S(2)}) copy-start(s32[2,384]{1,0:T(2,128)} %param.17) | copy-start | bytes 9220
  35.4 32.4 %copy-start.15 = (f32[3,32]{1,0:T(4,128)S(1)}, f32[3,32]{1,0:T(4,128)}, u32[]{:S(2)}) copy-start(f32[3,32]{1,0:T(4,128)} %param.16) | copy-start | bytes 1156
  35.4 34.0 %copy-start.9 = (f32[32,2048]{1,0:T(8,128)S(1)}, f32[32,2048]{1,0:T(8,128)}, u32[]{:S(2)}) copy-start(f32[32,2048]{1,0:T(8,128)} %param.14) | copy-start | bytes 786436
  35.4 218.3 %copy-start.17 = (s32[64,8]{0,1:T(8,128)S(1)}, s32[64,8]{0,1:T(8,128)}, u32[]{:S(2)}) copy-start(s32[64,8]{0,1:T(8,128)} %param.18) | copy-start | bytes 6148
  35.5 235.8 %collective-permute-start.19 = (bf16[3,1,32,16384]{3,2,1,0:T(8,128)(2,1)}, bf16[3,1,32,16384]{3,2,1,0:T(8,128)(2,1)}, u32[]{:S(2)}, u32[]{:S(2)}) collective-permute-start(bf16[3,1,32,16384]{3,2,1,0:T(8,128)(2,1)} %pad_maximum_fusion.3), channel_id=1, source_target_pairs={{1,0},{2,1},{3,2},{4,3},{5,4},{6,5},{7,6},{8,7},{9,8},{10,9},{11,1... | collective-permute-start | bytes 9437192 | tf_op jit(solution)/shard_map/ppermute | solution.py:18
  36.9 244.9 %collective-permute-start.18 = (bf16[3,1,32,16384]{3,2,1,0:T(8,128)(2,1)}, bf16[3,1,32,16384]{3,2,1,0:T(8,128)(2,1)}, u32[]{:S(2)}, u32[]{:S(2)}) collective-permute-start(bf16[3,1,32,16384]{3,2,1,0:T(8,128)(2,1)} %pad_maximum_fusion.3), channel_id=1, source_target_pairs={{0,1},{1,2},{2,3},{3,4},{4,5},{5,6},{6,7},{7,8},{8,9},{9,10},{10,1... | collective-permute-start | bytes 9437192 | tf_op jit(solution)/shard_map/ppermute | solution.py:17
  53.4 4.3 copy-start.5
  54.3 3.5 copy-start.6
  57.8 242.4 %collective-permute-start.3 = (bf16[3,1,64,16384]{3,2,1,0:T(8,128)(2,1)}, bf16[3,1,64,16384]{3,2,1,0:T(8,128)(2,1)}, u32[]{:S(2)}, u32[]{:S(2)}) collective-permute-start(bf16[3,1,64,16384]{3,2,1,0:T(8,128)(2,1)} %pad_maximum_fusion.2), channel_id=1, source_target_pairs={{1,0},{2,1},{3,2},{4,3},{5,4},{6,5},{7,6},{8,7},{9,8},{10,9},{11,1... | collective-permute-start | bytes 18874376 | tf_op jit(solution)/shard_map/ppermute | solution.py:18
  59.1 241.1 %collective-permute-start.2 = (bf16[3,1,64,16384]{3,2,1,0:T(8,128)(2,1)}, bf16[3,1,64,16384]{3,2,1,0:T(8,128)(2,1)}, u32[]{:S(2)}, u32[]{:S(2)}) collective-permute-start(bf16[3,1,64,16384]{3,2,1,0:T(8,128)(2,1)} %pad_maximum_fusion.2), channel_id=1, source_target_pairs={{0,1},{1,2},{2,3},{3,4},{4,5},{5,6},{6,7},{7,8},{8,9},{9,10},{10,1... | collective-permute-start | bytes 18874376 | tf_op jit(solution)/shard_map/ppermute | solution.py:17
  66.4 184.1 %collective-permute-start.7 = (f32[3,1,3,16384]{3,1,2,0:T(1,128)}, f32[3,1,3,16384]{3,1,2,0:T(1,128)}, u32[]{:S(2)}, u32[]{:S(2)}) collective-permute-start(f32[3,1,3,16384]{3,1,2,0:T(1,128)} %constant_dynamic-update-slice_fusion), channel_id=1, source_target_pairs={{1,0},{2,1},{3,2},{4,3},{5,4},{6,5},{7,6},{8,7},{9,8},{10,9},{11,1... | collective-permute-start | bytes 1769480 | tf_op jit(solution)/shard_map/ppermute | solution.py:18
  250.5 13.2 %collective-permute-start.6 = (f32[3,1,3,16384]{3,1,2,0:T(1,128)}, f32[3,1,3,16384]{3,1,2,0:T(1,128)S(1)}, u32[]{:S(2)}, u32[]{:S(2)}) collective-permute-start(f32[3,1,3,16384]{3,1,2,0:T(1,128)} %constant_dynamic-update-slice_fusion), channel_id=1, source_target_pairs={{0,1},{1,2},{2,3},{3,4},{4,5},{5,6},{6,7},{7,8},{8,9},{9,10},{10,1... | collective-permute-start | bytes 1769480 | tf_op jit(solution)/shard_map/ppermute | solution.py:17
  263.7 18.1 %copy-start.2 = (bf16[32,16384]{1,0:T(8,128)(2,1)S(1)}, bf16[32,16384]{1,0:T(8,128)(2,1)}, u32[]{:S(2)}) copy-start(bf16[32,16384]{1,0:T(8,128)(2,1)} %param.13) | copy-start | bytes 3145732
  263.7 18.2 %copy-start.8 = (bf16[1,1,32,16384]{3,2,1,0:T(8,128)(2,1)S(1)}, bf16[1,1,32,16384]{3,2,1,0:T(8,128)(2,1)}, u32[]{:S(2)}) copy-start(bf16[1,1,32,16384]{3,2,1,0:T(8,128)(2,1)} %copy-done.7) | copy-start | bytes 3145732
  263.7 513.5 %collective-permute-start.21 = (f32[1,1,3,2048]{3,2,1,0:T(4,128)}, f32[1,1,3,2048]{3,2,1,0:T(4,128)}, u32[]{:S(2)}, u32[]{:S(2)}) collective-permute-start(f32[1,1,3,2048]{3,2,1,0:T(4,128)} %bitcast.21), channel_id=1, source_target_pairs={{16,0},{32,16},{48,32},{64,48},{80,64},{96,80},{112,96},{17,1},{33... | collective-permute-start | bytes 73736 | tf_op jit(solution)/shard_map/ppermute | solution.py:18
  271.3 505.8 %collective-permute-start.20 = (f32[1,1,3,2048]{3,2,1,0:T(4,128)}, f32[1,1,3,2048]{3,2,1,0:T(4,128)}, u32[]{:S(2)}, u32[]{:S(2)}) collective-permute-start(f32[1,1,3,2048]{3,2,1,0:T(4,128)} %bitcast.21), channel_id=1, source_target_pairs={{0,16},{16,32},{32,48},{48,64},{64,80},{80,96},{96,112},{1,17},{17... | collective-permute-start | bytes 73736 | tf_op jit(solution)/shard_map/ppermute | solution.py:17
  311.8 12.0 %copy-start = (bf16[72,8,64,256]{3,2,1,0:T(8,128)(2,1)}, bf16[72,8,64,256]{3,2,1,0:T(8,128)(2,1)S(1)}, u32[]{:S(2)}) copy-start(bf16[72,8,64,256]{3,2,1,0:T(8,128)(2,1)S(1)} %copy.75) | copy-start | bytes 56623108
  734.9 66.7 %collective-permute-start.8 = (bf16[64,16384]{1,0:T(8,128)(2,1)}, bf16[64,16384]{1,0:T(8,128)(2,1)}, u32[]{:S(2)}, u32[]{:S(2)}) collective-permute-start(bf16[64,16384]{1,0:T(8,128)(2,1)} %get-tuple-element.115), channel_id=1, source_target_pairs={{17,0},{18,1},{19,2},{20,3},{21,4},{22,5},{23,6},{24,7},{25,8},{26... | collective-permute-start | bytes 6291464 | tf_op jit(solution)/shard_map/ppermute | solution.py:26
  736.2 72.4 %collective-permute-start.15 = (bf16[64,16384]{1,0:T(8,128)(2,1)}, bf16[64,16384]{1,0:T(8,128)(2,1)}, u32[]{:S(2)}, u32[]{:S(2)}) collective-permute-start(bf16[64,16384]{1,0:T(8,128)(2,1)} %get-tuple-element.116), channel_id=1, source_target_pairs={{0,17},{1,18},{2,19},{3,20},{4,21},{5,22},{6,23},{7,24},{8,25},{9,... | collective-permute-start | bytes 6291464 | tf_op jit(solution)/shard_map/ppermute | solution.py:26
  742.8 68.8 %collective-permute-start.14 = (bf16[64,16384]{1,0:T(8,128)(2,1)}, bf16[64,16384]{1,0:T(8,128)(2,1)}, u32[]{:S(2)}, u32[]{:S(2)}) collective-permute-start(bf16[64,16384]{1,0:T(8,128)(2,1)} %get-tuple-element.117), channel_id=1, source_target_pairs={{0,16},{1,17},{2,18},{3,19},{4,20},{5,21},{6,22},{7,23},{8,24},{9,... | collective-permute-start | bytes 6291464 | tf_op jit(solution)/shard_map/ppermute | solution.py:26
  744.9 29.0 %copy-start.1 = (f32[32,64,32]{2,1,0:T(8,128)S(1)}, f32[32,64,32]{2,1,0:T(8,128)}, u32[]{:S(2)}) copy-start(f32[32,64,32]{2,1,0:T(8,128)} %reshape.197) | copy-start | bytes 786436
  744.9 31.3 %copy-start.10 = (f32[3,32]{0,1:T(8,128)S(1)}, f32[3,32]{0,1:T(8,128)}, u32[]{:S(2)}) copy-start(f32[3,32]{0,1:T(8,128)} %copy.61) | copy-start | bytes 1156
  744.9 32.0 %copy-start.16 = (f32[3,32]{1,0:T(4,128)S(1)}, f32[3,32]{1,0:T(4,128)}, u32[]{:S(2)}) copy-start(f32[3,32]{1,0:T(4,128)} %param.16) | copy-start | bytes 1156
  744.9 32.0 %copy-start.19 = (s32[1,16]{1,0:T(1,128)S(1)}, s32[1,16]{1,0:T(1,128)}, u32[]{:S(2)}) copy-start(s32[1,16]{1,0:T(1,128)} %param.19) | copy-start | bytes 196
  744.9 32.0 %copy-start.14 = (s32[64,8]{0,1:T(8,128)S(1)}, s32[64,8]{0,1:T(8,128)}, u32[]{:S(2)}) copy-start(s32[64,8]{0,1:T(8,128)} %fusion.107) | copy-start | bytes 6148
  778.0 9.3 collective-permute-start.23
  779.3 8.0 collective-permute-start.22
  791.6 144.5 %collective-permute-start.13 = (bf16[64,16384]{1,0:T(8,128)(2,1)}, bf16[64,16384]{1,0:T(8,128)(2,1)}, u32[]{:S(2)}, u32[]{:S(2)}) collective-permute-start(bf16[64,16384]{1,0:T(8,128)(2,1)} %get-tuple-element.118), channel_id=1, source_target_pairs={{0,15},{1,16},{2,17},{3,18},{4,19},{5,20},{6,21},{7,22},{8,23},{9,... | collective-permute-start | bytes 6291464 | tf_op jit(solution)/shard_map/ppermute | solution.py:26
  799.7 136.4 %collective-permute-start.12 = (bf16[64,16384]{1,0:T(8,128)(2,1)}, bf16[64,16384]{1,0:T(8,128)(2,1)}, u32[]{:S(2)}, u32[]{:S(2)}) collective-permute-start(bf16[64,16384]{1,0:T(8,128)(2,1)} %get-tuple-element.119), channel_id=1, source_target_pairs={{0,1},{1,2},{2,3},{3,4},{4,5},{5,6},{6,7},{7,8},{8,9},{9,10},{10,1... | collective-permute-start | bytes 6291464 | tf_op jit(solution)/shard_map/ppermute | solution.py:26
  801.6 134.5 %collective-permute-start.11 = (bf16[64,16384]{1,0:T(8,128)(2,1)}, bf16[64,16384]{1,0:T(8,128)(2,1)}, u32[]{:S(2)}, u32[]{:S(2)}) collective-permute-start(bf16[64,16384]{1,0:T(8,128)(2,1)} %get-tuple-element.120), channel_id=1, source_target_pairs={{1,0},{2,1},{3,2},{4,3},{5,4},{6,5},{7,6},{8,7},{9,8},{10,9},{11,1... | collective-permute-start | bytes 6291464 | tf_op jit(solution)/shard_map/ppermute | solution.py:26
  808.6 127.5 %collective-permute-start.10 = (bf16[64,16384]{1,0:T(8,128)(2,1)}, bf16[64,16384]{1,0:T(8,128)(2,1)}, u32[]{:S(2)}, u32[]{:S(2)}) collective-permute-start(bf16[64,16384]{1,0:T(8,128)(2,1)} %get-tuple-element.121), channel_id=1, source_target_pairs={{15,0},{16,1},{17,2},{18,3},{19,4},{20,5},{21,6},{22,7},{23,8},{24... | collective-permute-start | bytes 6291464 | tf_op jit(solution)/shard_map/ppermute | solution.py:26
  811.6 124.5 %collective-permute-start.9 = (bf16[64,16384]{1,0:T(8,128)(2,1)}, bf16[64,16384]{1,0:T(8,128)(2,1)}, u32[]{:S(2)}, u32[]{:S(2)}) collective-permute-start(bf16[64,16384]{1,0:T(8,128)(2,1)} %get-tuple-element.122), channel_id=1, source_target_pairs={{16,0},{17,1},{18,2},{19,3},{20,4},{21,5},{22,6},{23,7},{24,8},{25... | collective-permute-start | bytes 6291464 | tf_op jit(solution)/shard_map/ppermute | solution.py:26
  814.1 8.4 copy-start.11
  814.1 8.4 copy-start.12
  814.1 8.4 copy-start.13
  925.7 9.2 copy-start.3
Sparse Core Ops, SparseCore 0:
  777.0 145.1 all-gather.1
where the time goes:
time: 964 us; the launch traced here: 953 us
  local copies, waits for them, and re-layouts  298 us (31%)
  waiting for transfers between devices  295 us (31%)
  matrix products  130 us (13%)
  other arithmetic  128 us (13%)
  starting transfers between devices  86.8 us (9%)
  between operations  14.2 us (1%)
    ppermute x8, waiting for transfers between devices, with_halo(): after = lax.ppermute(initial, axis, down)  197 us
    all_gather x1, waiting for transfers between devices, turned_gather(): result, at, outs = (lax.all_gather(both, axis, axis=0, tiled=True), 0, [])  87.4 us
    gather x12, local copies, waits for them, and re-layouts, near_step(): src_vectors = vectors_pool[s_hood, :, s_leaf, :]  83.9 us
    dot_general x12, matrix products, near_step(): jnp.einsum('bvs,bts->bvt', src_vectors, block, preferred_element_type=jnp...  83.5 us
    scatter-add x12, other arithmetic, near_step(): return (buffer.at[t_hood, :, t_leaf, :].add(partial_value), None)  77 us
    while x2, local copies, waits for them, and re-layouts, shards(): lax.scan(near_step, start, (tgt_hood, tgt_leaf, src_hood, src_leaf))  47.3 us
    ppermute x8, starting transfers between devices, with_halo(): before = lax.ppermute(last, axis, up)  41.9 us
    reshape x1, local copies, waits for them, and re-layouts, shards(): buffer = buffer.reshape(3, 3, vec_count, leaves * leaf_width)  40.3 us
  transfers between devices with their start and end apart: 25, of which 8 were waited for; matrix products, arithmetic and copies ran while one was open for 57% of the time, Pallas kernels for 0%

commit v1 on v0

--- a/solution.py
+++ b/solution.py
@@ -29,7 +29,13 @@
 def turned_gather(arrays, axis, dims):
     turned = [jnp.moveaxis(a, dim, 0) for a, dim in zip(arrays, dims)]
     both = jnp.concatenate([t.reshape(len(t), -1) for t in turned], axis=1)
-    result, at, outs = (lax.all_gather(both, axis, axis=0, tiled=True), 0, [])
+    result, at, outs = (
+        jnp.concatenate(
+            lax.all_to_all(jnp.stack([both] * lax.axis_size(axis)), axis, 0, 0), axis=0
+        ),
+        0,
+        [],
+    )
     for t, dim in zip(turned, dims):
         share = result[:, at : at + t[0].size].reshape(-1, *t.shape[1:])
         outs.append(jnp.moveaxis(share, 0, dim))

time: 964 us -> 919 us (0.953)
  waiting for transfers between devices: 295 us -> 198 us
  starting transfers between devices: 86.8 us -> 116 us
  other arithmetic: 128 us -> 145 us
  between operations: 14.2 us -> 0.81 us
  local copies, waits for them, and re-layouts: 298 us -> 310 us
    all_gather x1 -> x0, waiting for transfers between devices: 87.4 us -> none  [turned_gather(): result, at, outs = (lax.all_gather(both, axis, axis=0, tiled=True), 0, [])]
    ppermute x8, waiting for transfers between devices: 197 us -> 129 us  [with_halo(): after = lax.ppermute(initial, axis, down)]
    ppermute x8, waiting for transfers between devices: 0.02 us -> 55.6 us  [from_behind(): return lax.ppermute(block, axis, route)]
    all_to_all x0 -> x1, starting transfers between devices: none -> 14.9 us  [turned_gather(): lax.all_to_all(jnp.stack([both] * lax.axis_size(axis)), axis, 0, 0)]
    ppermute x8, starting transfers between devices: 41.9 us -> 56.4 us  [with_halo(): before = lax.ppermute(last, axis, up)]
  transfers between devices with their start and end apart: 25 -> 25, of which waited for: 8 -> 7; matrix products, arithmetic and copies ran while one was open for 57% -> 64% of each run, Pallas kernels for 0% -> 0%
where the time goes in v1:
time: 919 us; the launch traced here: 903 us
  local copies, waits for them, and re-layouts  310 us (34%)
  waiting for transfers between devices  198 us (22%)
  other arithmetic  145 us (16%)
  matrix products  132 us (14%)
  starting transfers between devices  116 us (13%)
    ppermute x8, waiting for transfers between devices, with_halo(): after = lax.ppermute(initial, axis, down)  129 us
    gather x12, local copies, waits for them, and re-layouts, near_step(): src_vectors = vectors_pool[s_hood, :, s_leaf, :]  83.9 us
    dot_general x12, matrix products, near_step(): jnp.einsum('bvs,bts->bvt', src_vectors, block, preferred_element_type=jnp...  83.5 us
    scatter-add x12, other arithmetic, near_step(): return (buffer.at[t_hood, :, t_leaf, :].add(partial_value), None)  77.3 us
    ppermute x8, starting transfers between devices, with_halo(): before = lax.ppermute(last, axis, up)  56.4 us
    ppermute x8, waiting for transfers between devices, from_behind(): return lax.ppermute(block, axis, route)  55.6 us
    while x2, local copies, waits for them, and re-layouts, shards(): lax.scan(near_step, start, (tgt_hood, tgt_leaf, src_hood, src_leaf))  47.3 us
    reshape x1, local copies, waits for them, and re-layouts, shards(): buffer = buffer.reshape(3, 3, vec_count, leaves * leaf_width)  40.3 us
  transfers between devices with their start and end apart: 25, of which 7 were waited for; matrix products, arithmetic and copies ran while one was open for 64% of the time, Pallas kernels for 0%

profile of v1, /device:TPU:1, one launch (start us, length us, event | category | flops | bytes accessed | tf_op | source)
XLA Modules:
  0.0 902.9 jit_solution(13842670834198463821)
XLA Ops:
  27.0 14.7 %collective-permute-done.1 = bf16[1,1,64,16384]{3,2,1,0:T(8,128)(2,1)S(1)} collective-permute-done((bf16[1,1,64,16384]{3,2,1,0:T(8,128)(2,1)}, bf16[1,1,64,16384]{3,2,1,0:T(8,128)(2,1)S(1)}, u32[]{:S(2)}, u32[]{:S(2)}) %collective-permute-start.1) | collective-permute-done | bytes 2097184 | tf_op jit(solution)/shard_map/ppermute | solution.py:18
  41.7 6.1 collective-permute-done
  54.3 6.7 collective-permute-start.2
  72.9 114.2 %collective-permute-done.23 = f32[3,1,3,2048]{3,2,1,0:T(4,128)} collective-permute-done((f32[3,1,3,2048]{3,2,1,0:T(4,128)}, f32[3,1,3,2048]{3,2,1,0:T(4,128)}, u32[]{:S(2)}, u32[]{:S(2)}) %collective-permute-start.23) | collective-permute-done | bytes 73760 | tf_op jit(solution)/shard_map/ppermute | solution.py:18
  199.2 6.3 gather_fusion.4
  205.5 24.6 %collective-permute-start.16 = (bf16[1,1,32,16384]{3,2,1,0:T(8,128)(2,1)S(1)}, bf16[1,1,32,16384]{3,2,1,0:T(8,128)(2,1)S(1)}, u32[]{:S(2)}, u32[]{:S(2)}) collective-permute-start(bf16[1,1,32,16384]{3,2,1,0:T(8,128)(2,1)S(1)} %bitcast.205), channel_id=1, source_target_pairs={{0,16},{16,32},{32,48},{48,64},{64,80},{80,96},{96,112},{1,17},{17... | collective-permute-start | bytes 3145736 | tf_op jit(solution)/shard_map/ppermute | solution.py:17
  235.9 5.9 collective-permute-done.16
  246.7 6.7 collective-permute-start.18
  253.4 11.9 %pad_maximum_fusion = bf16[3,3,64,16384]{3,2,1,0:T(8,128)(2,1)S(1)} fusion(bf16[3,1,64,16384]{3,2,1,0:T(8,128)(2,1)} %collective-permute-done.3, bf16[1,1,64,16384]{3,2,1,0:T(8,128)(2,1)S(1)} %collective-permute-done.1, bf16[1,1,64,16384]{3,2,1,0:T(8,128)(2,1)S(1)} %bitcast.212, bf16[1,1,64,16384]{3,2,1,0:T(8,128)(2,1)S(1)} %copy-done.9, ...), kind=kLoop, calls=%fused_computation.43 | loop fusion | flops 37748736 | bytes 37748736 | tf_op jit(solution)/shard_map/concatenate | solution.py:19
  269.8 12.0 %copy.79 = bf16[9,64,64,256]{3,1,2,0:T(8,128)(2,1)} copy(bf16[9,64,64,256]{3,2,1,0:T(8,128)(2,1)S(1)} %bitcast.195) | data formatting | bytes 37748736 | tf_op jit(solution)/shard_map/while | solution.py:116
  281.9 12.6 %broadcast_in_dim.26 = f32[9,64,64,256]{3,1,2,0:T(8,128)} broadcast(f32[]{:T(128)} %constant.129.clone.1), dimensions={} | broadcast | bytes 37748740 | tf_op jit(solution)/shard_map/broadcast_in_dim | solution.py:115
  294.5 312.4 %while.10 = (s32[]{:T(128)}, f32[9,64,64,256]{3,1,2,0:T(8,128)}, s32[12,32]{1,0:T(8,128)}, s32[12,32]{1,0:T(8,128)}, s32[12,32]{1,0:T(8,128)}, /*index=5*/s32[12...) while((s32[]{:T(128)}, f32[9,64,64,256]{3,1,2,0:T(8,128)}, ...), condition=%wide.region_2.3_spmd, body=%wide.region_0.2_spmd.sunk | while | flops 289932096 | bytes 12912617 | solution.py:116
  300.1 7.0 gather_fusion
  307.1 7.0 fusion.137
  314.1 6.5 scatter_fusion
  326.2 7.0 gather_fusion
  333.2 7.0 fusion.137
  340.1 6.5 scatter_fusion
  352.2 7.0 gather_fusion
  359.2 7.0 fusion.137
  366.2 6.4 scatter_fusion
  378.2 7.0 gather_fusion
  385.2 7.0 fusion.137
  392.2 6.4 scatter_fusion
  404.2 7.0 gather_fusion
  411.2 7.0 fusion.137
  418.2 6.5 scatter_fusion
  430.3 7.0 gather_fusion
  437.3 7.0 fusion.137
  444.2 6.5 scatter_fusion
  456.3 7.0 gather_fusion
  463.3 7.0 fusion.137
  470.3 6.4 scatter_fusion
  482.3 7.0 gather_fusion
  489.3 7.0 fusion.137
  496.3 6.4 scatter_fusion
  508.3 7.0 gather_fusion
  515.3 7.0 fusion.137
  522.3 6.5 scatter_fusion
  534.4 7.0 gather_fusion
  541.4 7.0 fusion.137
  548.3 6.4 scatter_fusion
  560.4 7.0 gather_fusion
  567.4 7.0 fusion.137
  574.3 6.5 scatter_fusion
  586.5 7.0 gather_fusion
  593.5 7.0 fusion.137
  600.5 6.5 scatter_fusion
  606.9 35.3 %copy.81 = f32[9,64,64,256]{3,2,1,0:T(8,128)} copy(f32[9,64,64,256]{3,1,2,0:T(8,128)} %get-tuple-element.47) | data formatting | bytes 75497472 | tf_op jit(solution)/shard_map/while | solution.py:116
  642.2 40.3 %reshape.198 = f32[3,3,64,16384]{3,2,1,0:T(8,128)} reshape(f32[9,64,64,256]{3,2,1,0:T(8,128)} %copy.81) | data formatting | bytes 75497472 | tf_op jit(solution)/shard_map/reshape | solution.py:117
  682.5 13.1 %convert.10 = bf16[3,3,64,16384]{3,2,1,0:T(8,128)(2,1)S(1)} convert(f32[3,3,64,16384]{3,2,1,0:T(8,128)} %reshape.198) | non-fusion elementwise | flops 9437184 | bytes 56623104 | tf_op jit(solution)/shard_map/convert.7
  695.6 5.9 slice_bitcast_fusion.8
  702.8 7.4 collective-permute-start.15
  712.1 8.3 pad_maximum_fusion.1
  720.4 10.5 %copy.105 = bf16[36,8,64,256]{3,2,1,0:T(8,128)(2,1)} copy(bf16[36,8,64,256]{3,1,2,0:T(8,128)(2,1)} %bitcast.198) | data formatting | bytes 18874368
  731.0 29.1 %convert_bitcast_fusion = bf16[9,64,64,32]{1,3,2,0:T(8,128)(2,1)} fusion(bf16[9,32,64,256]{3,2,1,0:T(8,128)(2,1)} %bitcast.203, bf16[9,64,64,256]{3,2,1,0:T(8,128)(2,1)} %bitcast.196), kind=kOutput, calls=%fused_computation.59 | convolution fusion | flops 605159424 | bytes 30670848 | tf_op jit(solution)/shard_map/nvil,nril->nvir/dot_general | solution.py:55
  764.1 14.9 %all-to-all-start = ((f32[128,32,67]{2,1,0:T(8,128)}), f32[128,32,67]{2,1,0:T(8,128)S(1)}, u32[]{:S(2)}, u32[]{:S(2)}) async-start(f32[128,32,67]{2,1,0:T(8,128)} %stack.2), calls=%async_computation | async-start | bytes 4194304 | tf_op jit(solution)/shard_map/all_to_all | solution.py:34
  779.0 7.5 collective-permute-start.13
  788.4 7.0 collective-permute-start.11
  802.9 8.4 gather_fusion.3
  811.3 13.3 %fusion.47 = f32[64,64,32]{1,2,0:T(8,128)} fusion(bf16[64,8,64,32]{2,3,1,0:T(8,128)(2,1)} %bitcast.200, f32[64,32]{1,0:T(8,128)S(1)} %copy-done.16, f32[64,8,32]{2,1,0:T(8,128)} %bitcast.228, f32[64,32]{1,0:T(8,128)S(1)} %copy-done.17, f32[64,8,32]{2,1,0:T(8,128)} %bitcast.227, f32[64,32]{1,0:T(8,128)S(1)} %copy-done.15, f32[64,8,32]{2,1,0:T(8,128)S(1)} %bitcast.226), kind=kOutput, calls=%fused_computation.88 | convolution fusion | flops 407371776 | bytes 2842624 | tf_op jit(solution)/shard_map/ifvs,ifst->ivt/dot_general | solution.py:132
  836.8 32.9 %collective-permute-done.13 = bf16[64,16384]{1,0:T(8,128)(2,1)} collective-permute-done((bf16[64,16384]{1,0:T(8,128)(2,1)}, bf16[64,16384]{1,0:T(8,128)(2,1)}, u32[]{:S(2)}, u32[]{:S(2)}) %collective-permute-start.13) | collective-permute-done | bytes 2097184 | tf_op jit(solution)/shard_map/ppermute | solution.py:26
  869.7 22.7 %collective-permute-done.11 = bf16[64,16384]{1,0:T(8,128)(2,1)} collective-permute-done((bf16[64,16384]{1,0:T(8,128)(2,1)}, bf16[64,16384]{1,0:T(8,128)(2,1)}, u32[]{:S(2)}, u32[]{:S(2)}) %collective-permute-start.11) | collective-permute-done | bytes 2097184 | tf_op jit(solution)/shard_map/ppermute | solution.py:26
  892.4 10.2 %fusion.37 = f32[64,16384]{1,0:T(8,128)} fusion(f32[64,16384]{1,0:T(8,128)S(1)} %bitcast.199, f32[3,3,64,16384]{3,2,1,0:T(8,128)} %reshape.198, bf16[64,16384]{1,0:T(8,128)(2,1)} %collective-permute-done.15, bf16[64,16384]{1,0:T(8,128)(2,1)} %collective-permute-done.14, bf16[64,16384]{1,0:T(8,128)(2,1)} %collective-permute-done.13, ...), kind=kLoop, calls=%fused_computation.69 | loop fusion | flops 17825792 | bytes 29360128 | tf_op jit(solution)/shard_map/add | solution.py:153
  (255 shorter events, 168.0 us)
Async XLA Ops:
  0.0 63.8 %collective-permute-start.21 = (f32[1,1,3,2048]{3,2,1,0:T(4,128)}, f32[1,1,3,2048]{3,2,1,0:T(4,128)S(1)}, u32[]{:S(2)}, u32[]{:S(2)}) collective-permute-start(f32[1,1,3,2048]{3,2,1,0:T(4,128)} %bitcast.222), channel_id=1, source_target_pairs={{16,0},{32,16},{48,32},{64,48},{80,64},{96,80},{112,96},{17,1},{33... | collective-permute-start | bytes 73736 | tf_op jit(solution)/shard_map/ppermute | solution.py:18
  3.3 65.4 %collective-permute-start.20 = (f32[1,1,3,2048]{3,2,1,0:T(4,128)}, f32[1,1,3,2048]{3,2,1,0:T(4,128)S(1)}, u32[]{:S(2)}, u32[]{:S(2)}) collective-permute-start(f32[1,1,3,2048]{3,2,1,0:T(4,128)} %bitcast.223), channel_id=1, source_target_pairs={{0,16},{16,32},{32,48},{48,64},{64,80},{80,96},{96,112},{1,17},{17... | collective-permute-start | bytes 73736 | tf_op jit(solution)/shard_map/ppermute | solution.py:17
  8.2 52.7 %collective-permute-start.5 = (f32[1,1,3,16384]{3,1,2,0:T(1,128)}, f32[1,1,3,16384]{3,1,2,0:T(1,128)}, u32[]{:S(2)}, u32[]{:S(2)}) collective-permute-start(f32[1,1,3,16384]{3,1,2,0:T(1,128)} %broadcast_in_dim.28), channel_id=1, source_target_pairs={{16,0},{32,16},{48,32},{64,48},{80,64},{96,80},{112,96},{17,1},{33... | collective-permute-start | bytes 589832 | tf_op jit(solution)/shard_map/ppermute | solution.py:18
  10.1 10.8 %collective-permute-start.4 = (f32[1,1,3,16384]{3,1,2,0:T(1,128)}, f32[1,1,3,16384]{3,1,2,0:T(1,128)S(1)}, u32[]{:S(2)}, u32[]{:S(2)}) collective-permute-start(f32[1,1,3,16384]{3,1,2,0:T(1,128)} %broadcast_in_dim.28), channel_id=1, source_target_pairs={{0,16},{16,32},{32,48},{48,64},{64,80},{80,96},{96,112},{1,17},{17... | collective-permute-start | bytes 589832 | tf_op jit(solution)/shard_map/ppermute | solution.py:17
  13.8 28.0 %collective-permute-start.1 = (bf16[1,1,64,16384]{3,2,1,0:T(8,128)(2,1)}, bf16[1,1,64,16384]{3,2,1,0:T(8,128)(2,1)S(1)}, u32[]{:S(2)}, u32[]{:S(2)}) collective-permute-start(bf16[1,1,64,16384]{3,2,1,0:T(8,128)(2,1)} %bitcast.209), channel_id=1, source_target_pairs={{16,0},{32,16},{48,32},{64,48},{80,64},{96,80},{112,96},{17,1},{33... | collective-permute-start | bytes 6291464 | tf_op jit(solution)/shard_map/ppermute | solution.py:18
  20.9 26.9 %collective-permute-start = (bf16[1,1,64,16384]{3,2,1,0:T(8,128)(2,1)}, bf16[1,1,64,16384]{3,2,1,0:T(8,128)(2,1)S(1)}, u32[]{:S(2)}, u32[]{:S(2)}) collective-permute-start(bf16[1,1,64,16384]{3,2,1,0:T(8,128)(2,1)} %bitcast.210), channel_id=1, source_target_pairs={{0,16},{16,32},{32,48},{48,64},{64,80},{80,96},{96,112},{1,17},{17... | collective-permute-start | bytes 6291464 | tf_op jit(solution)/shard_map/ppermute | solution.py:17
  27.0 41.7 %copy-start.12 = (f32[3,2048]{1,0:T(4,128)S(1)}, f32[3,2048]{1,0:T(4,128)}, u32[]{:S(2)}) copy-start(f32[3,2048]{1,0:T(4,128)} %param.15) | copy-start | bytes 73732
  27.0 43.7 %copy-start.22 = (s32[1,16]{1,0:T(1,128)S(1)}, s32[1,16]{1,0:T(1,128)}, u32[]{:S(2)}) copy-start(s32[1,16]{1,0:T(1,128)} %param.19) | copy-start | bytes 196
  27.0 43.7 %copy-start.18 = (f32[3,32]{1,0:T(4,128)S(1)}, f32[3,32]{1,0:T(4,128)}, u32[]{:S(2)}) copy-start(f32[3,32]{1,0:T(4,128)} %param.16) | copy-start | bytes 1156
  27.0 44.6 %copy-start.13 = (f32[32,2048]{1,0:T(8,128)S(1)}, f32[32,2048]{1,0:T(8,128)}, u32[]{:S(2)}) copy-start(f32[32,2048]{1,0:T(8,128)} %param.14) | copy-start | bytes 786436
  27.0 165.3 %copy-start.4 = (bf16[32,16384]{1,0:T(8,128)(2,1)S(1)}, bf16[32,16384]{1,0:T(8,128)(2,1)}, u32[]{:S(2)}) copy-start(bf16[32,16384]{1,0:T(8,128)(2,1)} %param.13) | copy-start | bytes 3145732
  47.8 5.2 copy-start.8
  53.0 200.4 %collective-permute-start.3 = (bf16[3,1,64,16384]{3,2,1,0:T(8,128)(2,1)}, bf16[3,1,64,16384]{3,2,1,0:T(8,128)(2,1)}, u32[]{:S(2)}, u32[]{:S(2)}) collective-permute-start(bf16[3,1,64,16384]{3,2,1,0:T(8,128)(2,1)} %pad_maximum_fusion.2), channel_id=1, source_target_pairs={{1,0},{2,1},{3,2},{4,3},{5,4},{6,5},{7,6},{8,7},{9,8},{10,9},{11,1... | collective-permute-start | bytes 18874376 | tf_op jit(solution)/shard_map/ppermute | solution.py:18
  54.3 199.1 %collective-permute-start.2 = (bf16[3,1,64,16384]{3,2,1,0:T(8,128)(2,1)}, bf16[3,1,64,16384]{3,2,1,0:T(8,128)(2,1)}, u32[]{:S(2)}, u32[]{:S(2)}) collective-permute-start(bf16[3,1,64,16384]{3,2,1,0:T(8,128)(2,1)} %pad_maximum_fusion.2), channel_id=1, source_target_pairs={{0,1},{1,2},{2,3},{3,4},{4,5},{5,6},{6,7},{7,8},{8,9},{9,10},{10,1... | collective-permute-start | bytes 18874376 | tf_op jit(solution)/shard_map/ppermute | solution.py:17
  62.6 142.9 %collective-permute-start.7 = (f32[3,1,3,16384]{3,1,2,0:T(1,128)}, f32[3,1,3,16384]{3,1,2,0:T(1,128)}, u32[]{:S(2)}, u32[]{:S(2)}) collective-permute-start(f32[3,1,3,16384]{3,1,2,0:T(1,128)} %constant_dynamic-update-slice_fusion), channel_id=1, source_target_pairs={{1,0},{2,1},{3,2},{4,3},{5,4},{6,5},{7,6},{8,7},{9,8},{10,9},{11,1... | collective-permute-start | bytes 1769480 | tf_op jit(solution)/shard_map/ppermute | solution.py:18
  63.9 166.2 %collective-permute-start.6 = (f32[3,1,3,16384]{3,1,2,0:T(1,128)}, f32[3,1,3,16384]{3,1,2,0:T(1,128)}, u32[]{:S(2)}, u32[]{:S(2)}) collective-permute-start(f32[3,1,3,16384]{3,1,2,0:T(1,128)} %constant_dynamic-update-slice_fusion), channel_id=1, source_target_pairs={{0,1},{1,2},{2,3},{3,4},{4,5},{5,6},{6,7},{7,8},{8,9},{9,10},{10,1... | collective-permute-start | bytes 1769480 | tf_op jit(solution)/shard_map/ppermute | solution.py:17
  69.3 117.8 %collective-permute-start.23 = (f32[3,1,3,2048]{3,2,1,0:T(4,128)}, f32[3,1,3,2048]{3,2,1,0:T(4,128)}, u32[]{:S(2)}, u32[]{:S(2)}) collective-permute-start(f32[3,1,3,2048]{3,2,1,0:T(4,128)} %pad_maximum_fusion.6), channel_id=1, source_target_pairs={{1,0},{2,1},{3,2},{4,3},{5,4},{6,5},{7,6},{8,7},{9,8},{10,9},{11,1... | collective-permute-start | bytes 221192 | tf_op jit(solution)/shard_map/ppermute | solution.py:18
  71.5 161.7 %copy-start = (s32[512]{0:T(512)}, s32[512]{0:T(512)S(1)}, u32[]{:S(2)}) copy-start(s32[512]{0:T(512)S(1)} %reshape.226) | copy-start | bytes 6148
  187.1 5.1 collective-permute-start.22
  192.2 43.6 %collective-permute-start.17 = (bf16[1,1,32,16384]{3,2,1,0:T(8,128)(2,1)S(1)}, bf16[1,1,32,16384]{3,2,1,0:T(8,128)(2,1)}, u32[]{:S(2)}, u32[]{:S(2)}) collective-permute-start(bf16[1,1,32,16384]{3,2,1,0:T(8,128)(2,1)S(1)} %bitcast.204), channel_id=1, source_target_pairs={{16,0},{32,16},{48,32},{64,48},{80,64},{96,80},{112,96},{17,1},{33... | collective-permute-start | bytes 3145736 | tf_op jit(solution)/shard_map/ppermute | solution.py:18
  205.5 36.3 %collective-permute-start.16 = (bf16[1,1,32,16384]{3,2,1,0:T(8,128)(2,1)S(1)}, bf16[1,1,32,16384]{3,2,1,0:T(8,128)(2,1)S(1)}, u32[]{:S(2)}, u32[]{:S(2)}) collective-permute-start(bf16[1,1,32,16384]{3,2,1,0:T(8,128)(2,1)S(1)} %bitcast.205), channel_id=1, source_target_pairs={{0,16},{16,32},{32,48},{48,64},{64,80},{80,96},{96,112},{1,17},{17... | collective-permute-start | bytes 3145736 | tf_op jit(solution)/shard_map/ppermute | solution.py:17
  235.9 17.5 %copy-start.7 = (bf16[64,16384]{1,0:T(8,128)(2,1)S(1)}, bf16[64,16384]{1,0:T(8,128)(2,1)}, u32[]{:S(2)}) copy-start(bf16[64,16384]{1,0:T(8,128)(2,1)} %param.12) | copy-start | bytes 6291460
  235.9 17.5 %copy-start.9 = (bf16[1,1,64,16384]{3,2,1,0:T(8,128)(2,1)S(1)}, bf16[1,1,64,16384]{3,2,1,0:T(8,128)(2,1)}, u32[]{:S(2)}) copy-start(bf16[1,1,64,16384]{3,2,1,0:T(8,128)(2,1)} %copy-done.8) | copy-start | bytes 6291460
  241.8 23.5 %copy-start.10 = (bf16[1,1,32,16384]{3,2,1,0:T(8,128)(2,1)}, bf16[1,1,32,16384]{3,2,1,0:T(8,128)(2,1)S(1)}, u32[]{:S(2)}) copy-start(bf16[1,1,32,16384]{3,2,1,0:T(8,128)(2,1)S(1)} %collective-permute-done.16) | copy-start | bytes 3145732
  245.4 466.7 %collective-permute-start.19 = (bf16[3,1,32,16384]{3,2,1,0:T(8,128)(2,1)}, bf16[3,1,32,16384]{3,2,1,0:T(8,128)(2,1)}, u32[]{:S(2)}, u32[]{:S(2)}) collective-permute-start(bf16[3,1,32,16384]{3,2,1,0:T(8,128)(2,1)} %pad_maximum_fusion.3), channel_id=1, source_target_pairs={{1,0},{2,1},{3,2},{4,3},{5,4},{6,5},{7,6},{8,7},{9,8},{10,9},{11,1... | collective-permute-start | bytes 9437192 | tf_op jit(solution)/shard_map/ppermute | solution.py:18
  246.7 465.4 %collective-permute-start.18 = (bf16[3,1,32,16384]{3,2,1,0:T(8,128)(2,1)}, bf16[3,1,32,16384]{3,2,1,0:T(8,128)(2,1)}, u32[]{:S(2)}, u32[]{:S(2)}) collective-permute-start(bf16[3,1,32,16384]{3,2,1,0:T(8,128)(2,1)} %pad_maximum_fusion.3), channel_id=1, source_target_pairs={{0,1},{1,2},{2,3},{3,4},{4,5},{5,6},{6,7},{7,8},{8,9},{9,10},{10,1... | collective-permute-start | bytes 9437192 | tf_op jit(solution)/shard_map/ppermute | solution.py:17
  269.8 12.0 %copy-start.2 = (bf16[72,8,64,256]{3,2,1,0:T(8,128)(2,1)}, bf16[72,8,64,256]{3,2,1,0:T(8,128)(2,1)S(1)}, u32[]{:S(2)}) copy-start(bf16[72,8,64,256]{3,2,1,0:T(8,128)(2,1)S(1)} %copy.104) | copy-start | bytes 56623108
  695.6 16.5 %copy-start.5 = (bf16[32,16384]{1,0:T(8,128)(2,1)S(1)}, bf16[32,16384]{1,0:T(8,128)(2,1)}, u32[]{:S(2)}) copy-start(bf16[32,16384]{1,0:T(8,128)(2,1)} %param.13) | copy-start | bytes 3145732
  695.6 16.5 %copy-start.11 = (bf16[1,1,32,16384]{3,2,1,0:T(8,128)(2,1)S(1)}, bf16[1,1,32,16384]{3,2,1,0:T(8,128)(2,1)}, u32[]{:S(2)}) copy-start(bf16[1,1,32,16384]{3,2,1,0:T(8,128)(2,1)} %copy-done.10) | copy-start | bytes 3145732
  701.5 86.9 %collective-permute-start.8 = (bf16[64,16384]{1,0:T(8,128)(2,1)}, bf16[64,16384]{1,0:T(8,128)(2,1)}, u32[]{:S(2)}, u32[]{:S(2)}) collective-permute-start(bf16[64,16384]{1,0:T(8,128)(2,1)} %get-tuple-element.131), channel_id=1, source_target_pairs={{17,0},{18,1},{19,2},{20,3},{21,4},{22,5},{23,6},{24,7},{25,8},{26... | collective-permute-start | bytes 6291464 | tf_op jit(solution)/shard_map/ppermute | solution.py:26
  702.8 92.6 %collective-permute-start.15 = (bf16[64,16384]{1,0:T(8,128)(2,1)}, bf16[64,16384]{1,0:T(8,128)(2,1)}, u32[]{:S(2)}, u32[]{:S(2)}) collective-permute-start(bf16[64,16384]{1,0:T(8,128)(2,1)} %get-tuple-element.132), channel_id=1, source_target_pairs={{0,17},{1,18},{2,19},{3,20},{4,21},{5,22},{6,23},{7,24},{8,25},{9,... | collective-permute-start | bytes 6291464 | tf_op jit(solution)/shard_map/ppermute | solution.py:26
  710.2 87.2 %collective-permute-start.14 = (bf16[64,16384]{1,0:T(8,128)(2,1)}, bf16[64,16384]{1,0:T(8,128)(2,1)}, u32[]{:S(2)}, u32[]{:S(2)}) collective-permute-start(bf16[64,16384]{1,0:T(8,128)(2,1)} %get-tuple-element.133), channel_id=1, source_target_pairs={{0,16},{1,17},{2,18},{3,19},{4,20},{5,21},{6,22},{7,23},{8,24},{9,... | collective-permute-start | bytes 6291464 | tf_op jit(solution)/shard_map/ppermute | solution.py:26
  731.0 29.1 %copy-start.3 = (f32[32,64,32]{2,1,0:T(8,128)S(1)}, f32[32,64,32]{2,1,0:T(8,128)}, u32[]{:S(2)}) copy-start(f32[32,64,32]{2,1,0:T(8,128)} %reshape.202) | copy-start | bytes 786436
  731.0 31.5 %copy-start.14 = (f32[3,32]{0,1:T(8,128)S(1)}, f32[3,32]{0,1:T(8,128)}, u32[]{:S(2)}) copy-start(f32[3,32]{0,1:T(8,128)} %copy.87) | copy-start | bytes 1156
  762.4 40.5 %copy-start.1 = (s32[512]{0:T(512)S(1)}, s32[512]{0:T(512)}, u32[]{:S(2)}) copy-start(s32[512]{0:T(512)} %copy-done) | copy-start | bytes 6148
  764.1 60.6 %all-to-all-start = ((f32[128,32,67]{2,1,0:T(8,128)}), f32[128,32,67]{2,1,0:T(8,128)S(1)}, u32[]{:S(2)}, u32[]{:S(2)}) async-start(f32[128,32,67]{2,1,0:T(8,128)} %stack.2), calls=%async_computation | async-start | bytes 4194304 | tf_op jit(solution)/shard_map/all_to_all | solution.py:34
  779.0 90.7 %collective-permute-start.13 = (bf16[64,16384]{1,0:T(8,128)(2,1)}, bf16[64,16384]{1,0:T(8,128)(2,1)}, u32[]{:S(2)}, u32[]{:S(2)}) collective-permute-start(bf16[64,16384]{1,0:T(8,128)(2,1)} %get-tuple-element.134), channel_id=1, source_target_pairs={{0,15},{1,16},{2,17},{3,18},{4,19},{5,20},{6,21},{7,22},{8,23},{9,... | collective-permute-start | bytes 6291464 | tf_op jit(solution)/shard_map/ppermute | solution.py:26
  786.5 83.2 %collective-permute-start.12 = (bf16[64,16384]{1,0:T(8,128)(2,1)}, bf16[64,16384]{1,0:T(8,128)(2,1)}, u32[]{:S(2)}, u32[]{:S(2)}) collective-permute-start(bf16[64,16384]{1,0:T(8,128)(2,1)} %get-tuple-element.135), channel_id=1, source_target_pairs={{0,1},{1,2},{2,3},{3,4},{4,5},{5,6},{6,7},{7,8},{8,9},{9,10},{10,1... | collective-permute-start | bytes 6291464 | tf_op jit(solution)/shard_map/ppermute | solution.py:26
  788.4 104.0 %collective-permute-start.11 = (bf16[64,16384]{1,0:T(8,128)(2,1)}, bf16[64,16384]{1,0:T(8,128)(2,1)}, u32[]{:S(2)}, u32[]{:S(2)}) collective-permute-start(bf16[64,16384]{1,0:T(8,128)(2,1)} %get-tuple-element.136), channel_id=1, source_target_pairs={{1,0},{2,1},{3,2},{4,3},{5,4},{6,5},{7,6},{8,7},{9,8},{10,9},{11,1... | collective-permute-start | bytes 6291464 | tf_op jit(solution)/shard_map/ppermute | solution.py:26
  795.4 97.0 %collective-permute-start.10 = (bf16[64,16384]{1,0:T(8,128)(2,1)}, bf16[64,16384]{1,0:T(8,128)(2,1)}, u32[]{:S(2)}, u32[]{:S(2)}) collective-permute-start(bf16[64,16384]{1,0:T(8,128)(2,1)} %get-tuple-element.137), channel_id=1, source_target_pairs={{15,0},{16,1},{17,2},{18,3},{19,4},{20,5},{21,6},{22,7},{23,8},{24... | collective-permute-start | bytes 6291464 | tf_op jit(solution)/shard_map/ppermute | solution.py:26
  797.3 95.1 %collective-permute-start.9 = (bf16[64,16384]{1,0:T(8,128)(2,1)}, bf16[64,16384]{1,0:T(8,128)(2,1)}, u32[]{:S(2)}, u32[]{:S(2)}) collective-permute-start(bf16[64,16384]{1,0:T(8,128)(2,1)} %get-tuple-element.138), channel_id=1, source_target_pairs={{16,0},{17,1},{18,2},{19,3},{20,4},{21,5},{22,6},{23,7},{24,8},{25... | collective-permute-start | bytes 6291464 | tf_op jit(solution)/shard_map/ppermute | solution.py:26
  802.9 8.4 copy-start.15
  802.9 8.4 copy-start.16
  802.9 8.4 copy-start.17
  824.7 7.6 copy-start.19
  824.7 7.6 copy-start.20
  824.7 7.6 copy-start.21
  830.4 5.2 copy-start.6
